TPU v7x, 512 devices: a whole 4x4x16 slice. The times are simulated.
512 devices in a mesh: dp: 128 (over z, x, core), mp: 4 (over y).
Axes of the slice: x: 4, y: 4, z: 16, core: 2. Of those that a mesh axis runs over, the one named last changes fastest.
Arguments:
- grad_blocks: bfloat16 [256, 128, 128], P('dp', None, 'mp'), may hold values from -0.5 to 0.5
- owner_table: int32 [256], replicated, may hold values from 0 to 127, as said below
- prev_stats: float32 [1024, 2, 128, 128], P('dp'), as said below
Outputs:
- update: bfloat16 [256, 128, 128], P('dp', None, 'mp')
- new_stats: float32 [1024, 2, 128, 128], P('dp')
- inv_roots: float32 [1024, 2, 128, 128], P('dp')
Inputs may be any that keep to these rules, and one draw needn't show every extreme that they name: `owner_table`: every entry is a dp index; no index appears more than 8 times, and some index appears exactly 8 times. `prev_stats`: each [128, 128] matrix is symmetric positive semidefinite.
All inputs are finite; a program needn't handle non-finite values.
Results may differ from a plain program's by a relative error of at most 0.001.
Values may be sent and summed in bfloat16 or wider, within the bound.
A program may use at most 64 MiB of HBM per device.

v0:
```python
import jax
import jax.numpy as jnp
from jax import lax
from jax.sharding import PartitionSpec as P

ITERS = 16
STAT_DECAY = 0.75
DAMPING = 0.03


def batch_product(first, second):
    return jnp.einsum("pij,pjk->pik", first, second, precision=lax.Precision.HIGHEST)


def newton_roots(matrices):
    width = matrices.shape[-1]
    identity = jnp.eye(width, dtype=jnp.float32)
    trace_val = jnp.trace(matrices, axis1=1, axis2=2)
    damped = matrices + DAMPING / width * trace_val[:, None, None] * identity
    norm_val = jnp.sqrt(jnp.sum(damped * damped, axis=(1, 2)))
    root_mat = identity * (1.0 / jnp.sqrt(jnp.sqrt(norm_val)))[:, None, None]
    remainder = damped / norm_val[:, None, None]

    def refine(unused, state_pair):
        root_now, rest_now = state_pair
        factor = (5.0 * identity - rest_now) * 0.25
        root_now = batch_product(root_now, factor)
        square = batch_product(factor, factor)
        quartic = batch_product(square, square)
        return (root_now, batch_product(quartic, rest_now))

    root_mat, remainder = lax.fori_loop(0, ITERS, refine, (root_mat, remainder))
    return root_mat


def per_device(grad_blocks, owner_table, prev_stats):
    dev_count = lax.axis_size("dp")
    my_index = lax.axis_index("dp")
    part_count = lax.axis_size("mp")
    part_index = lax.axis_index("mp")
    blk_local = grad_blocks.shape[0]
    width = grad_blocks.shape[1]
    part_width = grad_blocks.shape[2]
    capacity = prev_stats.shape[0]
    block_total = owner_table.shape[0]
    home_owner = lax.dynamic_slice_in_dim(owner_table, my_index * blk_local, blk_local)
    send_mask = jnp.arange(dev_count, dtype=jnp.int32)[:, None] == home_owner[None, :]
    owned_mask = (owner_table == my_index).astype(jnp.int32)
    slot_rank = jnp.cumsum(owned_mask) - owned_mask
    slot_range = jnp.arange(capacity, dtype=jnp.int32)
    picker = ((owned_mask[None, :] == 1) & (slot_rank[None, :] == slot_range[:, None])).astype(
        jnp.bfloat16
    )
    filled = slot_range < jnp.sum(owned_mask)

    def route(blocks):
        return jnp.where(send_mask[:, :, None, None], blocks[None], jnp.zeros((), blocks.dtype))

    def pick(arrived):
        flat = arrived.reshape(block_total, -1)
        chosen = jnp.dot(picker, flat, preferred_element_type=jnp.float32)
        return chosen.astype(jnp.bfloat16).reshape((capacity,) + arrived.shape[2:])

    arrived = lax.all_to_all(route(grad_blocks), "dp", split_axis=0, concat_axis=0, tiled=True)
    whole = lax.all_gather(pick(arrived), "mp", axis=2, tiled=True)
    left_stat = jnp.einsum("rik,rjk->rij", whole, whole, preferred_element_type=jnp.float32)
    right_stat = jnp.einsum("rki,rkj->rij", whole, whole, preferred_element_type=jnp.float32)
    blended = STAT_DECAY * prev_stats + (1.0 - STAT_DECAY) * jnp.stack(
        [left_stat, right_stat], axis=1
    )
    new_stats = jnp.where(filled[:, None, None, None], blended, 0.0)
    identity = jnp.eye(width, dtype=jnp.float32)
    problems = jnp.where(filled[:, None, None, None], blended, identity).reshape(
        2 * capacity, width, width
    )
    share = 2 * capacity // part_count
    my_problems = lax.dynamic_slice_in_dim(problems, part_index * share, share, 0)
    roots_flat = lax.all_gather(newton_roots(my_problems), "mp", axis=0, tiled=True)
    roots = roots_flat.reshape(capacity, 2, width, width)
    inv_roots = jnp.where(filled[:, None, None, None], roots, 0.0)
    whole_wide = whole.astype(jnp.float32)
    precond = jnp.einsum("rij,rjk->rik", roots[:, 0], whole_wide, precision=lax.Precision.HIGHEST)
    precond = jnp.einsum("rij,rjk->rik", precond, roots[:, 1], precision=lax.Precision.HIGHEST)
    spread = jnp.sqrt(jnp.mean(precond * precond, axis=(1, 2)))
    spread = jnp.where(filled, spread, 1.0)
    scaled = (precond / spread[:, None, None]).astype(jnp.bfloat16)
    columns = lax.dynamic_slice_in_dim(scaled, part_index * part_width, part_width, 2)
    outgoing = jnp.dot(picker.T, columns.reshape(capacity, -1), preferred_element_type=jnp.float32)
    outgoing = outgoing.astype(jnp.bfloat16).reshape(dev_count, blk_local, width, part_width)
    returned = lax.all_to_all(outgoing, "dp", split_axis=0, concat_axis=0, tiled=True)
    update = returned[home_owner, jnp.arange(blk_local, dtype=jnp.int32)]
    return (update, new_stats, inv_roots)


def solution(mesh):
    return jax.shard_map(
        per_device,
        mesh=mesh,
        in_specs=(P("dp", None, "mp"), P(), P("dp", None, None, None)),
        out_specs=(P("dp", None, "mp"), P("dp", None, None, None), P("dp", None, None, None)),
        check_vma=False,
    )
```

profile of v0, /device:TPU:33, one launch (start us, length us, event | category | flops | bytes accessed | tf_op | source)
XLA Modules:
  0.0 361.8 jit_solution(6509518457858769847)
XLA Ops:
  7.2 0.8 fusion.27
  7.9 2.3 broadcast_select_fusion
  10.2 19.4 %all-to-all-start = ((bf16[128,2,128,32]{2,3,1,0:T(8,128)(2,1)}), bf16[128,2,128,32]{2,3,1,0:T(8,128)(2,1)S(1)}, u32[]{:S(2)}, u32[]{:S(2)}) async-start(bf16[128,2,128,32]{2,3,1,0:T(8,128)(2,1)} %broadcast_select_fusion), calls=%async_computation | async-start | bytes 4194304 | tf_op jit(solution)/shard_map/all_to_all | solution.py:64
  30.3 0.6 fusion.28
  30.9 0.6 iota_compare_fusion.4
  31.6 97.5 %all-to-all-done = bf16[128,2,128,32]{2,3,1,0:T(8,128)(2,1)S(1)} async-done(((bf16[128,2,128,32]{2,3,1,0:T(8,128)(2,1)}), bf16[128,2,128,32]{2,3,1,0:T(8,128)(2,1)S(1)}, u32[]{:S(2)}, u32[]{:S(2)}) %all-to-all-start) | async-done | bytes 2097184 | tf_op jit(solution)/shard_map/all_to_all | solution.py:64
  129.1 6.5 %copy.32 = bf16[128,2,128,32]{3,2,1,0:T(8,128)(2,1)} copy(bf16[128,2,128,32]{2,3,1,0:T(8,128)(2,1)S(1)} %all-to-all-done) | data formatting | bytes 4194304 | tf_op jit(solution)/shard_map/all_to_all | solution.py:64
  135.6 10.7 %reshape.97 = bf16[256,4096]{1,0:T(8,128)(2,1)S(1)} reshape(bf16[128,2,128,32]{3,2,1,0:T(8,128)(2,1)} %copy.32) | data formatting | bytes 4194304 | tf_op jit(solution)/shard_map/reshape | solution.py:60
  146.9 10.7 %all_gather.6 = bf16[8,128,128]{1,2,0:T(8,128)(2,1)S(1)} all-gather(bf16[8,128,32]{1,2,0:T(8,128)(2,1)S(1)} %copy.33), channel_id=1, replica_groups=mesh['dp'=128,'mp'=4] {'mp'}, dimensions={2}, use_global_device_ids=true | all-gather | bytes 327680 | tf_op jit(solution)/shard_map/all_gather | solution.py:65
  159.2 29.6 %while.13 = (s32[]{:T(128)}, f32[4,128,128]{1,2,0:T(8,128)S(1)}, f32[4,128,128]{2,1,0:T(8,128)S(1)}, s32[]{:T(128)}) while((s32[]{:T(128)}, f32[4,128,128]{1,2,0:T(8,128)S(1)}, f32[4,128,128]{2,1,0:T(8,128)S(1)}, s32[]{:T(128)}) %tuple.39), condition=%wide.region_6.7_spmd.clone, body=%wide.region_5.6_spmd.clone.sunk | while | flops 402948096 | bytes 3866677 | solution.py:32
  160.1 0.6 convolution_bitcast_fusion.4
  161.9 0.6 convolution_bitcast_fusion.4
  163.8 0.6 convolution_bitcast_fusion.4
  164.4 0.4 fusion.64
  165.6 0.6 convolution_bitcast_fusion.4
  166.2 0.4 fusion.64
  167.5 0.6 convolution_bitcast_fusion.4
  169.3 0.6 convolution_bitcast_fusion.4
  169.9 0.4 fusion.64
  171.1 0.6 convolution_bitcast_fusion.4
  171.8 0.4 fusion.64
  173.0 0.6 convolution_bitcast_fusion.4
  174.8 0.6 convolution_bitcast_fusion.4
  176.7 0.6 convolution_bitcast_fusion.4
  177.3 0.4 fusion.64
  178.5 0.6 convolution_bitcast_fusion.4
  180.4 0.6 convolution_bitcast_fusion.4
  181.0 0.4 fusion.64
  182.2 0.6 convolution_bitcast_fusion.4
  184.1 0.6 convolution_bitcast_fusion.4
  185.9 0.6 convolution_bitcast_fusion.4
  187.8 0.6 convolution_bitcast_fusion.4
  188.4 0.4 fusion.64
  188.8 0.8 copy.36
  189.7 23.8 %all-gather.2.cloned.1.call-done = f32[16,128,128]{2,1,0:T(8,128)} async-done(((f32[4,128,128]{2,1,0:T(8,128)}), f32[16,128,128]{2,1,0:T(8,128)}) %all-gather.2.cloned.1.call-update) | async-done | bytes 1048592 | tf_op jit(solution)/shard_map/all_gather | solution.py:78
  213.5 2.5 broadcast_select_fusion.1
  215.9 0.7 fusion.12
  216.6 1.1 multiply_reduce_fusion
  217.7 0.7 sqrt_select_fusion
  218.9 0.8 convolution_convert_fusion
  219.7 8.0 %reshape.102 = bf16[128,2,128,32]{3,2,1,0:T(8,128)(2,1)} reshape(bf16[256,4096]{1,0:T(8,128)(2,1)S(1)} %convolution_convert_fusion) | data formatting | bytes 4194304 | tf_op jit(solution)/shard_map/reshape | solution.py:89
  227.7 7.9 %copy.40 = bf16[128,2,128,32]{2,3,1,0:T(8,128)(2,1)} copy(bf16[128,2,128,32]{3,2,1,0:T(8,128)(2,1)} %reshape.102) | data formatting | bytes 4194304 | tf_op jit(solution)/shard_map/reshape | solution.py:89
  235.6 18.8 %all-to-all-start.1 = ((bf16[128,2,128,32]{2,3,1,0:T(8,128)(2,1)}), bf16[128,2,128,32]{2,3,1,0:T(8,128)(2,1)S(1)}, u32[]{:S(2)}, u32[]{:S(2)}) async-start(bf16[128,2,128,32]{2,3,1,0:T(8,128)(2,1)} %copy.40), calls=%async_computation.1 | async-start | bytes 4194304 | tf_op jit(solution)/shard_map/all_to_all | solution.py:90
  254.4 1.0 copy.42
  255.4 0.6 copy-done
  256.0 1.1 copy.43
  257.1 96.8 %all-to-all-done.1 = bf16[128,2,128,32]{2,3,1,0:T(8,128)(2,1)S(1)} async-done(((bf16[128,2,128,32]{2,3,1,0:T(8,128)(2,1)}), bf16[128,2,128,32]{2,3,1,0:T(8,128)(2,1)S(1)}, u32[]{:S(2)}, u32[]{:S(2)}) %all-to-all-start.1) | async-done | bytes 2097184 | tf_op jit(solution)/shard_map/all_to_all | solution.py:90
  353.8 1.2 gather_fusion
  (122 shorter events, 19.5 us)
Async XLA Ops:
  10.2 19.5 %copy-start.3 = (s32[256]{0:T(256)S(1)}, s32[256]{0:T(256)}, u32[]{:S(2)}) copy-start(s32[256]{0:T(256)} %param.6) | copy-start | bytes 3076
  10.2 118.8 %all-to-all-start = ((bf16[128,2,128,32]{2,3,1,0:T(8,128)(2,1)}), bf16[128,2,128,32]{2,3,1,0:T(8,128)(2,1)S(1)}, u32[]{:S(2)}, u32[]{:S(2)}) async-start(bf16[128,2,128,32]{2,3,1,0:T(8,128)(2,1)} %broadcast_select_fusion), calls=%async_computation | async-start | bytes 4194304 | tf_op jit(solution)/shard_map/all_to_all | solution.py:64
  29.7 183.8 %all-gather.2.cloned.1.call-start = ((), (), s32[]{:S(2)}) async-start(), calls=%async_computation.2 | async-start | bytes 1310720 | tf_op jit(solution)/shard_map/all_gather | solution.py:78
  146.2 12.0 %copy-start.2 = (f32[8,2,128,128]{3,2,1,0:T(8,128)S(1)}, f32[8,2,128,128]{3,2,1,0:T(8,128)}, u32[]{:S(2)}) copy-start(f32[8,2,128,128]{3,2,1,0:T(8,128)} %param.7) | copy-start | bytes 3145732
  213.5 3.1 copy-start.1
  235.6 118.2 %all-to-all-start.1 = ((bf16[128,2,128,32]{2,3,1,0:T(8,128)(2,1)}), bf16[128,2,128,32]{2,3,1,0:T(8,128)(2,1)S(1)}, u32[]{:S(2)}, u32[]{:S(2)}) async-start(bf16[128,2,128,32]{2,3,1,0:T(8,128)(2,1)} %copy.40), calls=%async_computation.1 | async-start | bytes 4194304 | tf_op jit(solution)/shard_map/all_to_all | solution.py:90
  254.4 1.6 copy-start
Sparse Core Ops, SparseCore 0:
  189.8 23.6 all-gather.1
where the time goes:
time: 363 us; the launch traced here: 362 us
  waiting for transfers between devices  218 us (60%)
  local copies, waits for them, and re-layouts  39.5 us (11%)
  starting transfers between devices  38.2 us (11%)
  matrix products  31.2 us (9%)
  between operations  14.2 us (4%)
  blocking collectives  10.7 us (3%)
  other arithmetic  8.89 us (2%)
    all_to_all x1, waiting for transfers between devices, per_device(): lax.all_to_all(route(grad_blocks), 'dp', split_axis=0, concat_axis=0, til...  97.5 us
    all_to_all x1, waiting for transfers between devices, per_device(): lax.all_to_all(outgoing, 'dp', split_axis=0, concat_axis=0, tiled=True)  96.8 us
    dot_general x64, matrix products, batch_product(): jnp.einsum('pij,pjk->pik', first, second, precision=lax.Precision.HIGHEST)  27.7 us
    all_gather x1, waiting for transfers between devices, per_device(): lax.all_gather(newton_roots(my_problems), 'mp', axis=0, tiled=True)  23.8 us
    all_to_all x1, starting transfers between devices, per_device(): lax.all_to_all(route(grad_blocks), 'dp', split_axis=0, concat_axis=0, til...  19.4 us
    all_to_all x1, starting transfers between devices, per_device(): lax.all_to_all(outgoing, 'dp', split_axis=0, concat_axis=0, tiled=True)  18.8 us
    reshape x2, local copies, waits for them, and re-layouts, per_device(): outgoing.astype(jnp.bfloat16)  15.9 us
    all_gather x1, blocking collectives, per_device(): whole = lax.all_gather(pick(arrived), 'mp', axis=2, tiled=True)  10.7 us
  transfers between devices with their start and end apart: 3, of which 3 were waited for; matrix products, arithmetic and copies ran while one was open for 1% of the time, Pallas kernels for 0%

commit v1 on v0

--- a/solution.py
+++ b/solution.py
@@ -75,7 +75,15 @@
     )
     share = 2 * capacity // part_count
     my_problems = lax.dynamic_slice_in_dim(problems, part_index * share, share, 0)
-    roots_flat = lax.all_gather(newton_roots(my_problems), "mp", axis=0, tiled=True)
+    roots_flat = jnp.concatenate(
+        lax.all_to_all(
+            jnp.stack(lax.axis_size("mp") * [newton_roots(my_problems)], axis=0),
+            axis_name="mp",
+            split_axis=0,
+            concat_axis=0,
+        ),
+        axis=0,
+    )
     roots = roots_flat.reshape(capacity, 2, width, width)
     inv_roots = jnp.where(filled[:, None, None, None], roots, 0.0)
     whole_wide = whole.astype(jnp.float32)

time: 363 us -> 332 us (0.915)
  between operations: 14.2 us -> 0.84 us
  waiting for transfers between devices: 218 us -> 208 us
  starting transfers between devices: 38.2 us -> 32.2 us
    all_gather x1 -> x0, waiting for transfers between devices: 23.8 us -> none  [per_device(): lax.all_gather(newton_roots(my_problems), 'mp', axis=0, tiled=True)]
    all_to_all x0 -> x1, waiting for transfers between devices: none -> 13.4 us  [per_device(): lax.all_to_all(jnp.stack(lax.axis_size('mp') * [newton_roots(my_problems)...]
    all_to_all x1, starting transfers between devices: 18.8 us -> 9.29 us  [per_device(): lax.all_to_all(outgoing, 'dp', split_axis=0, concat_axis=0, tiled=True)]
where the time goes in v1:
time: 332 us; the launch traced here: 331 us
  waiting for transfers between devices  208 us (63%)
  local copies, waits for them, and re-layouts  39.9 us (12%)
  starting transfers between devices  32.2 us (10%)
  matrix products  31.2 us (9%)
  blocking collectives  10.7 us (3%)
  other arithmetic  7.59 us (2%)
    all_to_all x1, waiting for transfers between devices, per_device(): lax.all_to_all(route(grad_blocks), 'dp', split_axis=0, concat_axis=0, til...  97.5 us
    all_to_all x1, waiting for transfers between devices, per_device(): lax.all_to_all(outgoing, 'dp', split_axis=0, concat_axis=0, tiled=True)  96.8 us
    dot_general x64, matrix products, batch_product(): jnp.einsum('pij,pjk->pik', first, second, precision=lax.Precision.HIGHEST)  27.7 us
    all_to_all x1, starting transfers between devices, per_device(): lax.all_to_all(route(grad_blocks), 'dp', split_axis=0, concat_axis=0, til...  19.4 us
    reshape x2, local copies, waits for them, and re-layouts, per_device(): outgoing.astype(jnp.bfloat16)  15.9 us
    all_to_all x1, waiting for transfers between devices, per_device(): lax.all_to_all(jnp.stack(lax.axis_size('mp') * [newton_roots(my_problems)...  13.4 us
    all_gather x1, blocking collectives, per_device(): whole = lax.all_gather(pick(arrived), 'mp', axis=2, tiled=True)  10.7 us
    reshape x1, local copies, waits for them, and re-layouts, pick(): flat = arrived.reshape(block_total, -1)  10.7 us
  transfers between devices with their start and end apart: 3, of which 3 were waited for; matrix products, arithmetic and copies ran while one was open for 1% of the time, Pallas kernels for 0%

profile of v1, /device:TPU:33, one launch (start us, length us, event | category | flops | bytes accessed | tf_op | source)
XLA Modules:
  0.0 331.1 jit_solution(344616469350821097)
XLA Ops:
  0.6 0.8 fusion.27
  1.4 2.3 broadcast_select_fusion
  3.7 19.4 %all-to-all-start = ((bf16[128,2,128,32]{2,3,1,0:T(8,128)(2,1)}), bf16[128,2,128,32]{2,3,1,0:T(8,128)(2,1)S(1)}, u32[]{:S(2)}, u32[]{:S(2)}) async-start(bf16[128,2,128,32]{2,3,1,0:T(8,128)(2,1)} %broadcast_select_fusion), calls=%async_computation | async-start | bytes 4194304 | tf_op jit(solution)/shard_map/all_to_all | solution.py:64
  23.7 0.6 fusion.28
  24.3 0.6 iota_compare_fusion.4
  25.0 97.5 %all-to-all-done = bf16[128,2,128,32]{2,3,1,0:T(8,128)(2,1)S(1)} async-done(((bf16[128,2,128,32]{2,3,1,0:T(8,128)(2,1)}), bf16[128,2,128,32]{2,3,1,0:T(8,128)(2,1)S(1)}, u32[]{:S(2)}, u32[]{:S(2)}) %all-to-all-start) | async-done | bytes 2097184 | tf_op jit(solution)/shard_map/all_to_all | solution.py:64
  122.6 6.5 %copy.33 = bf16[128,2,128,32]{3,2,1,0:T(8,128)(2,1)} copy(bf16[128,2,128,32]{2,3,1,0:T(8,128)(2,1)S(1)} %all-to-all-done) | data formatting | bytes 4194304 | tf_op jit(solution)/shard_map/all_to_all | solution.py:64
  129.0 10.7 %reshape.96 = bf16[256,4096]{1,0:T(8,128)(2,1)S(1)} reshape(bf16[128,2,128,32]{3,2,1,0:T(8,128)(2,1)} %copy.33) | data formatting | bytes 4194304 | tf_op jit(solution)/shard_map/reshape | solution.py:60
  140.4 10.7 %all_gather.3 = bf16[8,128,128]{1,2,0:T(8,128)(2,1)S(1)} all-gather(bf16[8,128,32]{1,2,0:T(8,128)(2,1)S(1)} %copy.34), channel_id=1, replica_groups=mesh['dp'=128,'mp'=4] {'mp'}, dimensions={2}, use_global_device_ids=true | all-gather | bytes 327680 | tf_op jit(solution)/shard_map/all_gather | solution.py:65
  152.7 29.6 %while.13 = (s32[]{:T(128)}, f32[4,128,128]{1,2,0:T(8,128)S(1)}, f32[4,128,128]{2,1,0:T(8,128)S(1)}, s32[]{:T(128)}) while((s32[]{:T(128)}, f32[4,128,128]{1,2,0:T(8,128)S(1)}, f32[4,128,128]{2,1,0:T(8,128)S(1)}, s32[]{:T(128)}) %tuple.39), condition=%wide.region_6.7_spmd.clone, body=%wide.region_5.6_spmd.clone.sunk | while | flops 402948096 | bytes 3866677 | solution.py:32
  153.5 0.6 convolution_bitcast_fusion.4
  154.1 0.4 fusion.63
  155.4 0.6 convolution_bitcast_fusion.4
  156.0 0.4 fusion.63
  157.2 0.6 convolution_bitcast_fusion.4
  159.1 0.6 convolution_bitcast_fusion.4
  160.9 0.6 convolution_bitcast_fusion.4
  161.5 0.4 fusion.63
  162.8 0.6 convolution_bitcast_fusion.4
  164.6 0.6 convolution_bitcast_fusion.4
  166.4 0.6 convolution_bitcast_fusion.4
  167.1 0.4 fusion.63
  168.3 0.6 convolution_bitcast_fusion.4
  170.1 0.6 convolution_bitcast_fusion.4
  170.8 0.4 fusion.63
  172.0 0.6 convolution_bitcast_fusion.4
  173.8 0.6 convolution_bitcast_fusion.4
  175.7 0.6 convolution_bitcast_fusion.4
  177.5 0.6 convolution_bitcast_fusion.4
  178.1 0.4 fusion.63
  179.4 0.6 convolution_bitcast_fusion.4
  181.2 0.6 convolution_bitcast_fusion.4
  182.4 1.1 stack.19
  183.5 3.5 %all-to-all-start.1 = ((f32[4,4,128,128]{3,2,1,0:T(8,128)}), f32[4,4,128,128]{3,2,1,0:T(8,128)S(1)}, u32[]{:S(2)}, u32[]{:S(2)}) async-start(f32[4,4,128,128]{3,2,1,0:T(8,128)} %stack.19), calls=%async_computation.1 | async-start | bytes 2097152 | tf_op jit(solution)/shard_map/all_to_all | solution.py:79
  187.0 13.4 %all-to-all-done.1 = f32[4,4,128,128]{3,2,1,0:T(8,128)S(1)} async-done(((f32[4,4,128,128]{3,2,1,0:T(8,128)}), f32[4,4,128,128]{3,2,1,0:T(8,128)S(1)}, u32[]{:S(2)}, u32[]{:S(2)}) %all-to-all-start.1) | async-done | bytes 1048608 | tf_op jit(solution)/shard_map/all_to_all | solution.py:79
  200.4 1.2 broadcast_select_fusion.1
  201.5 0.7 fusion.12
  202.2 1.1 multiply_reduce_fusion
  203.3 0.7 sqrt_select_fusion
  204.5 0.8 convolution_convert_fusion
  205.3 8.0 %reshape.100 = bf16[128,2,128,32]{3,2,1,0:T(8,128)(2,1)} reshape(bf16[256,4096]{1,0:T(8,128)(2,1)S(1)} %convolution_convert_fusion) | data formatting | bytes 4194304 | tf_op jit(solution)/shard_map/reshape | solution.py:97
  213.3 7.9 %copy.41 = bf16[128,2,128,32]{2,3,1,0:T(8,128)(2,1)} copy(bf16[128,2,128,32]{3,2,1,0:T(8,128)(2,1)} %reshape.100) | data formatting | bytes 4194304 | tf_op jit(solution)/shard_map/reshape | solution.py:97
  221.2 9.3 %all-to-all-start.2 = ((bf16[128,2,128,32]{2,3,1,0:T(8,128)(2,1)}), bf16[128,2,128,32]{2,3,1,0:T(8,128)(2,1)S(1)}, u32[]{:S(2)}, u32[]{:S(2)}) async-start(bf16[128,2,128,32]{2,3,1,0:T(8,128)(2,1)} %copy.41), calls=%async_computation.2 | async-start | bytes 4194304 | tf_op jit(solution)/shard_map/all_to_all | solution.py:98
  230.5 1.1 copy.43
  231.6 0.5 copy-done
  232.1 1.1 copy.44
  233.2 96.8 %all-to-all-done.2 = bf16[128,2,128,32]{2,3,1,0:T(8,128)(2,1)S(1)} async-done(((bf16[128,2,128,32]{2,3,1,0:T(8,128)(2,1)}), bf16[128,2,128,32]{2,3,1,0:T(8,128)(2,1)S(1)}, u32[]{:S(2)}, u32[]{:S(2)}) %all-to-all-start.2) | async-done | bytes 2097184 | tf_op jit(solution)/shard_map/all_to_all | solution.py:98
  329.9 1.2 gather_fusion
  (120 shorter events, 20.0 us)
Async XLA Ops:
  3.7 19.4 %copy-start.2 = (s32[256]{0:T(256)S(1)}, s32[256]{0:T(256)}, u32[]{:S(2)}) copy-start(s32[256]{0:T(256)} %param.6) | copy-start | bytes 3076
  3.7 118.8 %all-to-all-start = ((bf16[128,2,128,32]{2,3,1,0:T(8,128)(2,1)}), bf16[128,2,128,32]{2,3,1,0:T(8,128)(2,1)S(1)}, u32[]{:S(2)}, u32[]{:S(2)}) async-start(bf16[128,2,128,32]{2,3,1,0:T(8,128)(2,1)} %broadcast_select_fusion), calls=%async_computation | async-start | bytes 4194304 | tf_op jit(solution)/shard_map/all_to_all | solution.py:64
  140.1 11.6 %copy-start.1 = (f32[8,2,128,128]{3,2,1,0:T(8,128)S(1)}, f32[8,2,128,128]{3,2,1,0:T(8,128)}, u32[]{:S(2)}) copy-start(f32[8,2,128,128]{3,2,1,0:T(8,128)} %param.7) | copy-start | bytes 3145732
  183.5 16.9 %all-to-all-start.1 = ((f32[4,4,128,128]{3,2,1,0:T(8,128)}), f32[4,4,128,128]{3,2,1,0:T(8,128)S(1)}, u32[]{:S(2)}, u32[]{:S(2)}) async-start(f32[4,4,128,128]{3,2,1,0:T(8,128)} %stack.19), calls=%async_computation.1 | async-start | bytes 2097152 | tf_op jit(solution)/shard_map/all_to_all | solution.py:79
  221.2 108.7 %all-to-all-start.2 = ((bf16[128,2,128,32]{2,3,1,0:T(8,128)(2,1)}), bf16[128,2,128,32]{2,3,1,0:T(8,128)(2,1)S(1)}, u32[]{:S(2)}, u32[]{:S(2)}) async-start(bf16[128,2,128,32]{2,3,1,0:T(8,128)(2,1)} %copy.41), calls=%async_computation.2 | async-start | bytes 4194304 | tf_op jit(solution)/shard_map/all_to_all | solution.py:98
  230.5 1.6 copy-start
